TPU v7x, 32 devices: a whole 2x2x4 slice. The times are simulated.
32 devices in a mesh: groups: 2 (over y), tensor: 4 (over z), section: 4 (over x, core).
Axes of the slice: x: 2, y: 2, z: 4, core: 2. Of those that a mesh axis runs over, the one named last changes fastest.
Arguments:
- hidden: bfloat16 [16, 8192], P('groups', 'tensor'), parts along dimension 0, may hold values from -6 to 6
- norm_gain: bfloat16 [4, 8192], P('section'), may hold values from 0.5 to 1.5
- query_weight: bfloat16 [4, 8192, 512], P('section', None, 'tensor'), may hold values from -0.0625 to 0.0625
- query_bias: bfloat16 [4, 512], P('section', 'tensor'), may hold values from -10 to 10
- kv_weight: bfloat16 [4, 8192, 1024], P('section', None, 'tensor'), may hold values from -0.0625 to 0.0625
- out_weight: bfloat16 [4, 512, 8192], P('section', None, 'tensor'), may hold values from -0.25 to 0.25
- kv_pool: bfloat16 [4, 48, 16, 1024], P('section', ('groups', 'tensor')), parts along dimension 1, may hold values from -8 to 8
- page_table: int32 [16, 4], P(('groups', 'tensor')), parts along dimension 0, may hold values from 0 to 23, as said below
- context_len: int32 [16], P(('groups', 'tensor')), parts along dimension 0, may hold values from 33 to 64, as said below
Outputs:
- result: bfloat16 [16, 8192], P(('groups', 'section'), 'tensor'), parts along dimension 0
There are 2 independent parts, one for each index of `groups`. A program takes and returns all parts, laid end to end along the dimension named above; an argument that names none is the same for every part. Nothing has to cross between parts.
Inputs may be any that keep to these rules, and one draw needn't show every extreme that they name: `page_table`: sample r belongs to block k = r // 2; its 4 pages lie in k * 6 to (k + 1) * 6 - 1. The first 2 pages are the same for all samples of a block, every other page belongs to one sample only. `context_len`: some sample has 64 cached tokens.
All inputs are finite; a program needn't handle non-finite values.
Results may differ from a plain program's by a relative error of at most 0.018.
Values may be sent and summed in bfloat16 or wider, within the bound.
A program may use at most 64 MiB of HBM per device.

v0:
```python
import jax
import jax.numpy as jnp
from jax import lax
from jax.sharding import PartitionSpec as P

HD = 128
KVH = 4


epsilon = 1e-06
rope_base = 1000000.0


def shifted(value, axis, steps):
    count = lax.axis_size(axis)
    initial, last = (max(0, -steps), min(count, count - steps))
    return lax.ppermute(value, axis, [(source, source + steps) for source in range(initial, last)])


def rotate(values, position):
    head_size = values.shape[-1]
    half_size = head_size // 2
    frequency = rope_base ** (-(jnp.arange(half_size, dtype=jnp.float32) * 2.0) / head_size)
    angles = position.astype(jnp.float32)[:, None] * frequency[None, :]
    cosine = jnp.cos(angles)[:, None, :]
    sine_part = jnp.sin(angles)[:, None, :]
    front_half = values[..., :half_size]
    back_half = values[..., half_size:]
    return jnp.concatenate(
        [front_half * cosine - back_half * sine_part, back_half * cosine + front_half * sine_part],
        axis=-1,
    )


def attend(queries, key_new, value_new, cached, position):
    row_count, head_count, head_size = queries.shape
    kv_heads = key_new.shape[1]
    group_size = head_count // kv_heads
    span_len = cached.shape[1]
    keys_all = cached[:, :, : kv_heads * head_size].reshape(
        row_count, span_len, kv_heads, head_size
    )
    values_all = cached[:, :, kv_heads * head_size :].reshape(
        row_count, span_len, kv_heads, head_size
    )
    grouped = queries.reshape(row_count, kv_heads, group_size, head_size)
    scaling = head_size ** (-0.5)
    scores = (
        jnp.einsum("rkgd,rskd->rkgs", grouped, keys_all, preferred_element_type=jnp.float32)
        * scaling
    )
    own_score = (
        jnp.einsum("rkgd,rkd->rkg", grouped, key_new, preferred_element_type=jnp.float32) * scaling
    )
    usable = (jnp.arange(span_len, dtype=jnp.int32)[None, :] < position[:, None])[:, None, None, :]
    row_max = jnp.maximum(jnp.max(jnp.where(usable, scores, -1e30), axis=-1), own_score)
    weights = jnp.where(usable, jnp.exp(scores - row_max[..., None]), 0.0)
    own_weight = jnp.exp(own_score - row_max)
    denominator = jnp.sum(weights, axis=-1) + own_weight
    weights = (weights / denominator[..., None]).astype(jnp.bfloat16)
    own_weight = (own_weight / denominator).astype(jnp.bfloat16)
    mixture = jnp.einsum("rkgs,rskd->rkgd", weights, values_all, preferred_element_type=jnp.float32)
    mixture = (
        mixture
        + own_weight.astype(jnp.float32)[..., None] * value_new.astype(jnp.float32)[:, :, None, :]
    )
    return mixture.reshape(row_count, head_count * head_size).astype(jnp.bfloat16)


def shards(
    hidden,
    norm_gain,
    query_weight,
    query_bias,
    kv_weight,
    out_weight,
    kv_pool,
    page_table,
    context_len,
):
    slot_count = lax.axis_size("tensor")
    section_count = lax.axis_size("section")
    section_id = lax.axis_index("section")
    tensor_id = lax.axis_index("tensor")
    row_total, width_dev = hidden.shape
    row_dev = row_total // slot_count
    pool_pages = kv_pool.shape[1]
    gain_row = norm_gain[0].astype(jnp.float32)
    query_proj = query_weight[0]
    bias_row = query_bias[0].astype(jnp.float32)
    kv_proj = kv_weight[0]
    out_proj = out_weight[0]
    pool_layer = kv_pool[0]
    local_pages = page_table - tensor_id * pool_pages
    pieces = 1
    per_piece = row_dev // pieces
    tick_count = section_count + pieces - 1
    is_first = section_id == 0
    finished = [None] * pieces
    carried = jnp.zeros((slot_count * per_piece, width_dev), jnp.bfloat16)
    for tick_index in range(tick_count):
        if tick_index < pieces:
            blocks = hidden.reshape(slot_count, row_dev, hidden.shape[1])
            carried = jnp.where(
                is_first, blocks.reshape(slot_count * per_piece, hidden.shape[1]), carried
            )
        whole = lax.all_gather(carried, "tensor", axis=1, tiled=True)
        wide_rows = whole.astype(jnp.float32)
        mean_sq = jnp.mean(wide_rows * wide_rows, axis=1, keepdims=True)
        normed = (wide_rows * lax.rsqrt(mean_sq + epsilon) * gain_row).astype(jnp.bfloat16)
        queries = (
            jnp.dot(normed, query_proj, preferred_element_type=jnp.float32) + bias_row
        ).astype(jnp.bfloat16)
        fresh_kv = jnp.dot(normed, kv_proj, preferred_element_type=jnp.float32).astype(jnp.bfloat16)
        query_rows = lax.all_to_all(queries, "tensor", split_axis=0, concat_axis=1, tiled=True)
        fresh_rows = lax.all_to_all(fresh_kv, "tensor", split_axis=0, concat_axis=1, tiled=True)
        cached = pool_layer[local_pages].reshape(per_piece, -1, pool_layer.shape[-1])
        rotated = rotate(
            query_rows.reshape(per_piece, -1, HD).astype(jnp.float32), context_len
        ).astype(jnp.bfloat16)
        key_new = rotate(
            fresh_rows[:, : KVH * HD].reshape(per_piece, KVH, HD).astype(jnp.float32), context_len
        ).astype(jnp.bfloat16)
        value_new = fresh_rows[:, KVH * HD :].reshape(per_piece, KVH, HD)
        mixture = attend(rotated, key_new, value_new, cached, context_len)
        carried = (
            carried.astype(jnp.float32)
            + jnp.dot(
                lax.all_gather(mixture, "tensor", axis=0, tiled=True),
                out_proj,
                preferred_element_type=jnp.float32,
            )
        ).astype(jnp.bfloat16)
        if tick_index >= section_count - 1:
            finished[tick_index - section_count + 1] = carried
        if tick_index < tick_count - 1:
            carried = shifted(carried, "section", 1)
    stacked = jnp.concatenate(
        [done_part.reshape(slot_count, per_piece, width_dev) for done_part in finished], axis=1
    )
    result = stacked.reshape(row_total, width_dev)
    is_last = section_id == section_count - 1
    outgoing = jnp.where(is_last, result, jnp.zeros_like(result))[None]
    spread = lax.all_to_all(outgoing, "section", split_axis=1, concat_axis=0, tiled=True)
    return spread[section_count - 1]


def solution(mesh):
    return jax.shard_map(
        shards,
        mesh=mesh,
        in_specs=(
            P("groups", "tensor"),
            P("section", None),
            P("section", None, "tensor"),
            P("section", "tensor"),
            P("section", None, "tensor"),
            P("section", None, "tensor"),
            P("section", ("groups", "tensor"), None, None),
            P(("groups", "tensor"), None),
            P(("groups", "tensor")),
        ),
        out_specs=P(("groups", "section"), "tensor"),
        check_vma=False,
    )
```

profile of v0, /device:TPU:0, one launch (start us, length us, event | category | flops | bytes accessed | tf_op | source)
XLA Modules:
  0.0 216.4 jit_solution(4219618170490121716)
XLA Ops:
  0.9 15.1 %all_gather.24 = bf16[8,8192]{1,0:T(8,128)(2,1)S(1)} all-gather(bf16[8,2048]{1,0:T(8,128)(2,1)S(1)} %broadcast_select_fusion), channel_id=1, replica_groups=mesh['groups'=2,'tensor'=4,'section'=4] {'tensor'}, dimensions={1}, use_global_device_ids=true | all-gather | bytes 163840 | tf_op jit(solution)/shard_map/all_gather | solution.py:107
  20.3 4.7 %all-to-all-start = ((bf16[4,2,128]{2,1,0:T(2,128)(2,1)}), bf16[4,2,128]{2,1,0:T(2,128)(2,1)S(1)}, u32[]{:S(2)}, u32[]{:S(2)}) async-start(bf16[4,2,128]{2,1,0:T(2,128)(2,1)} %bitcast.3), calls=%async_computation | async-start | bytes 4096 | tf_op jit(solution)/shard_map/all_to_all | solution.py:115
  25.7 2.9 %fusion.24 = bf16[8,256]{1,0:T(8,128)(2,1)S(1)} fusion(bf16[1,8192,256]{2,1,0:T(8,128)(2,1)} %param.13, bf16[8,8192]{1,0:T(8,128)(2,1)S(1)} %all_gather.24, f32[8192]{0:T(1024)S(1)} %bitcast.175, f32[8]{0:T(128)S(1)} %add_rsqrt_fusion.3), kind=kOutput, calls=%fused_computation.26 | convolution fusion | flops 33818624 | bytes 4362272 | tf_op jit(solution)/shard_map/dot_general | solution.py:114
  30.4 4.1 %all-to-all-start.1 = ((bf16[4,2,256]{2,1,0:T(2,128)(2,1)}), bf16[4,2,256]{2,1,0:T(2,128)(2,1)S(1)}, u32[]{:S(2)}, u32[]{:S(2)}) async-start(bf16[4,2,256]{2,1,0:T(2,128)(2,1)} %all_to_all.107), calls=%async_computation.1 | async-start | bytes 8192 | tf_op jit(solution)/shard_map/all_to_all | solution.py:116
  34.5 5.6 %all-to-all-done.1 = bf16[4,2,256]{2,1,0:T(2,128)(2,1)S(1)} async-done(((bf16[4,2,256]{2,1,0:T(2,128)(2,1)}), bf16[4,2,256]{2,1,0:T(2,128)(2,1)S(1)}, u32[]{:S(2)}, u32[]{:S(2)}) %all-to-all-start.1) | async-done | bytes 4128 | tf_op jit(solution)/shard_map/all_to_all | solution.py:116
  41.3 11.9 %all-gather = bf16[4,2,512]{2,1,0:T(2,128)(2,1)S(1)} all-gather(bf16[1,2,512]{2,1,0:T(2,128)(2,1)S(1)} %reshape.429), channel_id=1, replica_groups=mesh['groups'=2,'tensor'=4,'section'=4] {'tensor'}, dimensions={0}, use_global_device_ids=true | all-gather | bytes 10240 | tf_op jit(solution)/shard_map/all_gather | solution.py:129
  55.9 13.6 %all_gather.26 = bf16[8,8192]{1,0:T(8,128)(2,1)S(1)} all-gather(bf16[8,2048]{1,0:T(8,128)(2,1)S(1)} %collective-permute-done), channel_id=1, replica_groups=mesh['groups'=2,'tensor'=4,'section'=4] {'tensor'}, dimensions={1}, use_global_device_ids=true | all-gather | bytes 163840 | tf_op jit(solution)/shard_map/all_gather | solution.py:107
  70.7 3.2 %all-to-all-start.2 = ((bf16[4,2,128]{2,1,0:T(2,128)(2,1)}), bf16[4,2,128]{2,1,0:T(2,128)(2,1)S(1)}, u32[]{:S(2)}, u32[]{:S(2)}) async-start(bf16[4,2,128]{2,1,0:T(2,128)(2,1)} %bitcast.20), calls=%async_computation.2 | async-start | bytes 4096 | tf_op jit(solution)/shard_map/all_to_all | solution.py:115
  74.0 2.9 %fusion.27 = bf16[8,256]{1,0:T(8,128)(2,1)S(1)} fusion(bf16[1,8192,256]{2,1,0:T(8,128)(2,1)} %param.13, bf16[8,8192]{1,0:T(8,128)(2,1)S(1)} %all_gather.26, f32[8]{0:T(128)S(1)} %add_rsqrt_fusion.2, f32[8192]{0:T(1024)S(1)} %bitcast.177), kind=kOutput, calls=%fused_computation.27 | convolution fusion | flops 33818624 | bytes 4362272 | tf_op jit(solution)/shard_map/dot_general | solution.py:114
  79.4 3.2 %all-to-all-start.3 = ((bf16[4,2,256]{2,1,0:T(2,128)(2,1)}), bf16[4,2,256]{2,1,0:T(2,128)(2,1)S(1)}, u32[]{:S(2)}, u32[]{:S(2)}) async-start(bf16[4,2,256]{2,1,0:T(2,128)(2,1)} %all_to_all.113), calls=%async_computation.3 | async-start | bytes 8192 | tf_op jit(solution)/shard_map/all_to_all | solution.py:116
  82.6 5.5 %all-to-all-done.3 = bf16[4,2,256]{2,1,0:T(2,128)(2,1)S(1)} async-done(((bf16[4,2,256]{2,1,0:T(2,128)(2,1)}), bf16[4,2,256]{2,1,0:T(2,128)(2,1)S(1)}, u32[]{:S(2)}, u32[]{:S(2)}) %all-to-all-start.3) | async-done | bytes 4128 | tf_op jit(solution)/shard_map/all_to_all | solution.py:116
  89.4 11.9 %all-gather.1 = bf16[4,2,512]{2,1,0:T(2,128)(2,1)S(1)} all-gather(bf16[1,2,512]{2,1,0:T(2,128)(2,1)S(1)} %reshape.431), channel_id=1, replica_groups=mesh['groups'=2,'tensor'=4,'section'=4] {'tensor'}, dimensions={0}, use_global_device_ids=true | all-gather | bytes 10240 | tf_op jit(solution)/shard_map/all_gather | solution.py:129
  104.0 13.4 %all_gather.28 = bf16[8,8192]{1,0:T(8,128)(2,1)S(1)} all-gather(bf16[8,2048]{1,0:T(8,128)(2,1)S(1)} %collective-permute-done.1), channel_id=1, replica_groups=mesh['groups'=2,'tensor'=4,'section'=4] {'tensor'}, dimensions={1}, use_global_device_ids=true | all-gather | bytes 163840 | tf_op jit(solution)/shard_map/all_gather | solution.py:107
  118.7 3.2 %all-to-all-start.4 = ((bf16[4,2,128]{2,1,0:T(2,128)(2,1)}), bf16[4,2,128]{2,1,0:T(2,128)(2,1)S(1)}, u32[]{:S(2)}, u32[]{:S(2)}) async-start(bf16[4,2,128]{2,1,0:T(2,128)(2,1)} %bitcast.33), calls=%async_computation.4 | async-start | bytes 4096 | tf_op jit(solution)/shard_map/all_to_all | solution.py:115
  127.3 3.2 %all-to-all-start.5 = ((bf16[4,2,256]{2,1,0:T(2,128)(2,1)}), bf16[4,2,256]{2,1,0:T(2,128)(2,1)S(1)}, u32[]{:S(2)}, u32[]{:S(2)}) async-start(bf16[4,2,256]{2,1,0:T(2,128)(2,1)} %all_to_all.119), calls=%async_computation.5 | async-start | bytes 8192 | tf_op jit(solution)/shard_map/all_to_all | solution.py:116
  130.6 5.5 %all-to-all-done.5 = bf16[4,2,256]{2,1,0:T(2,128)(2,1)S(1)} async-done(((bf16[4,2,256]{2,1,0:T(2,128)(2,1)}), bf16[4,2,256]{2,1,0:T(2,128)(2,1)S(1)}, u32[]{:S(2)}, u32[]{:S(2)}) %all-to-all-start.5) | async-done | bytes 4128 | tf_op jit(solution)/shard_map/all_to_all | solution.py:116
  137.3 11.9 %all-gather.2 = bf16[4,2,512]{2,1,0:T(2,128)(2,1)S(1)} all-gather(bf16[1,2,512]{2,1,0:T(2,128)(2,1)S(1)} %reshape.433), channel_id=1, replica_groups=mesh['groups'=2,'tensor'=4,'section'=4] {'tensor'}, dimensions={0}, use_global_device_ids=true | all-gather | bytes 10240 | tf_op jit(solution)/shard_map/all_gather | solution.py:129
  151.8 13.6 %all_gather.30 = bf16[8,8192]{1,0:T(8,128)(2,1)S(1)} all-gather(bf16[8,2048]{1,0:T(8,128)(2,1)S(1)} %collective-permute-done.2), channel_id=1, replica_groups=mesh['groups'=2,'tensor'=4,'section'=4] {'tensor'}, dimensions={1}, use_global_device_ids=true | all-gather | bytes 163840 | tf_op jit(solution)/shard_map/all_gather | solution.py:107
  168.2 3.2 %all-to-all-start.6 = ((bf16[4,2,128]{2,1,0:T(2,128)(2,1)}), bf16[4,2,128]{2,1,0:T(2,128)(2,1)S(1)}, u32[]{:S(2)}, u32[]{:S(2)}) async-start(bf16[4,2,128]{2,1,0:T(2,128)(2,1)} %bitcast.46), calls=%async_computation.6 | async-start | bytes 4096 | tf_op jit(solution)/shard_map/all_to_all | solution.py:115
  171.5 2.9 %fusion.33 = bf16[8,256]{1,0:T(8,128)(2,1)S(1)} fusion(bf16[1,8192,256]{2,1,0:T(8,128)(2,1)} %param.13, bf16[8,8192]{1,0:T(8,128)(2,1)S(1)} %all_gather.30, f32[8]{0:T(128)S(1)} %add_rsqrt_fusion, f32[8192]{0:T(1024)S(1)} %bitcast.181), kind=kOutput, calls=%fused_computation.29 | convolution fusion | flops 33818624 | bytes 4362272 | tf_op jit(solution)/shard_map/dot_general | solution.py:114
  176.9 3.2 %all-to-all-start.7 = ((bf16[4,2,256]{2,1,0:T(2,128)(2,1)}), bf16[4,2,256]{2,1,0:T(2,128)(2,1)S(1)}, u32[]{:S(2)}, u32[]{:S(2)}) async-start(bf16[4,2,256]{2,1,0:T(2,128)(2,1)} %all_to_all.125), calls=%async_computation.7 | async-start | bytes 8192 | tf_op jit(solution)/shard_map/all_to_all | solution.py:116
  180.1 5.5 %all-to-all-done.7 = bf16[4,2,256]{2,1,0:T(2,128)(2,1)S(1)} async-done(((bf16[4,2,256]{2,1,0:T(2,128)(2,1)}), bf16[4,2,256]{2,1,0:T(2,128)(2,1)S(1)}, u32[]{:S(2)}, u32[]{:S(2)}) %all-to-all-start.7) | async-done | bytes 4128 | tf_op jit(solution)/shard_map/all_to_all | solution.py:116
  186.9 11.9 %all-gather.3 = bf16[4,2,512]{2,1,0:T(2,128)(2,1)S(1)} all-gather(bf16[1,2,512]{2,1,0:T(2,128)(2,1)S(1)} %reshape.435), channel_id=1, replica_groups=mesh['groups'=2,'tensor'=4,'section'=4] {'tensor'}, dimensions={0}, use_global_device_ids=true | all-gather | bytes 10240 | tf_op jit(solution)/shard_map/all_gather | solution.py:129
  200.7 14.9 %all_to_all.140 = bf16[4,2,2048]{2,1,0:T(2,128)(2,1)S(1)} all-to-all(bf16[4,2,2048]{2,1,0:T(2,128)(2,1)S(1)} %reshape.466), channel_id=1, replica_groups=mesh['groups'=2,'tensor'=4,'section'=4] {'section'}, dimensions={0} | all-to-all | bytes 65536 | tf_op jit(solution)/shard_map/all_to_all | solution.py:144
  (131 shorter events, 38.7 us)
Async XLA Ops:
  0.0 53.2 %copy-start = (bf16[1,512,2048]{2,1,0:T(8,128)(2,1)S(1)}, bf16[1,512,2048]{2,1,0:T(8,128)(2,1)}, u32[]{:S(2)}) copy-start(bf16[1,512,2048]{2,1,0:T(8,128)(2,1)} %param.14) | copy-start | bytes 6291460
  0.0 25.0 %copy-start.4 = (s32[2,4]{1,0:T(2,128)S(1)}, s32[2,4]{1,0:T(2,128)}, u32[]{:S(2)}) copy-start(s32[2,4]{1,0:T(2,128)} %param.16) | copy-start | bytes 100
  0.0 25.1 %copy-start.3 = (bf16[1,6,16,1024]{3,2,1,0:T(8,128)(2,1)S(1)}, bf16[1,6,16,1024]{3,2,1,0:T(8,128)(2,1)}, u32[]{:S(2)}) copy-start(bf16[1,6,16,1024]{3,2,1,0:T(8,128)(2,1)} %param.15) | copy-start | bytes 589828
  20.3 10.1 %all-to-all-start = ((bf16[4,2,128]{2,1,0:T(2,128)(2,1)}), bf16[4,2,128]{2,1,0:T(2,128)(2,1)S(1)}, u32[]{:S(2)}, u32[]{:S(2)}) async-start(bf16[4,2,128]{2,1,0:T(2,128)(2,1)} %bitcast.3), calls=%async_computation | async-start | bytes 4096 | tf_op jit(solution)/shard_map/all_to_all | solution.py:115
  25.7 2.9 %copy-start.5 = (s32[2]{0:T(128)S(1)}, s32[2]{0:T(128)}, u32[]{:S(2)}) copy-start(s32[2]{0:T(128)} %param.17) | copy-start | bytes 28
  30.4 9.7 %all-to-all-start.1 = ((bf16[4,2,256]{2,1,0:T(2,128)(2,1)}), bf16[4,2,256]{2,1,0:T(2,128)(2,1)S(1)}, u32[]{:S(2)}, u32[]{:S(2)}) async-start(bf16[4,2,256]{2,1,0:T(2,128)(2,1)} %all_to_all.107), calls=%async_computation.1 | async-start | bytes 8192 | tf_op jit(solution)/shard_map/all_to_all | solution.py:116
  53.2 16.5 %copy-start.1 = (bf16[1,8192,128]{2,1,0:T(8,128)(2,1)S(1)}, bf16[1,8192,128]{2,1,0:T(8,128)(2,1)}, u32[]{:S(2)}) copy-start(bf16[1,8192,128]{2,1,0:T(8,128)(2,1)} %param.11) | copy-start | bytes 6291460
  53.6 2.3 %collective-permute-start = (bf16[8,2048]{1,0:T(8,128)(2,1)S(1)}, bf16[8,2048]{1,0:T(8,128)(2,1)S(1)}, u32[]{:S(2)}, u32[]{:S(2)}) collective-permute-start(bf16[8,2048]{1,0:T(8,128)(2,1)S(1)} %fusion.8), channel_id=1, source_target_pairs={{0,1},{1,2},{2,3},{4,5},{5,6},{6,7},{8,9},{9,10},{10,11},{12,13},{... | collective-permute-start | bytes 98312 | tf_op jit(solution)/shard_map/ppermute | solution.py:17
  70.7 8.6 %all-to-all-start.2 = ((bf16[4,2,128]{2,1,0:T(2,128)(2,1)}), bf16[4,2,128]{2,1,0:T(2,128)(2,1)S(1)}, u32[]{:S(2)}, u32[]{:S(2)}) async-start(bf16[4,2,128]{2,1,0:T(2,128)(2,1)} %bitcast.20), calls=%async_computation.2 | async-start | bytes 4096 | tf_op jit(solution)/shard_map/all_to_all | solution.py:115
  79.4 8.8 %all-to-all-start.3 = ((bf16[4,2,256]{2,1,0:T(2,128)(2,1)}), bf16[4,2,256]{2,1,0:T(2,128)(2,1)S(1)}, u32[]{:S(2)}, u32[]{:S(2)}) async-start(bf16[4,2,256]{2,1,0:T(2,128)(2,1)} %all_to_all.113), calls=%async_computation.3 | async-start | bytes 8192 | tf_op jit(solution)/shard_map/all_to_all | solution.py:116
  101.4 16.3 %copy-start.2 = (bf16[1,8192,128]{2,1,0:T(8,128)(2,1)S(1)}, bf16[1,8192,128]{2,1,0:T(8,128)(2,1)}, u32[]{:S(2)}) copy-start(bf16[1,8192,128]{2,1,0:T(8,128)(2,1)} %param.11) | copy-start | bytes 6291460
  101.8 2.3 %collective-permute-start.1 = (bf16[8,2048]{1,0:T(8,128)(2,1)S(1)}, bf16[8,2048]{1,0:T(8,128)(2,1)S(1)}, u32[]{:S(2)}, u32[]{:S(2)}) collective-permute-start(bf16[8,2048]{1,0:T(8,128)(2,1)S(1)} %add_convert_fusion.2), channel_id=1, source_target_pairs={{0,1},{1,2},{2,3},{4,5},{5,6},{6,7},{8,9},{9,10},{10,11},{12,13},{... | collective-permute-start | bytes 98312 | tf_op jit(solution)/shard_map/ppermute | solution.py:17
  118.7 8.6 %all-to-all-start.4 = ((bf16[4,2,128]{2,1,0:T(2,128)(2,1)}), bf16[4,2,128]{2,1,0:T(2,128)(2,1)S(1)}, u32[]{:S(2)}, u32[]{:S(2)}) async-start(bf16[4,2,128]{2,1,0:T(2,128)(2,1)} %bitcast.33), calls=%async_computation.4 | async-start | bytes 4096 | tf_op jit(solution)/shard_map/all_to_all | solution.py:115
  127.3 8.8 %all-to-all-start.5 = ((bf16[4,2,256]{2,1,0:T(2,128)(2,1)}), bf16[4,2,256]{2,1,0:T(2,128)(2,1)S(1)}, u32[]{:S(2)}, u32[]{:S(2)}) async-start(bf16[4,2,256]{2,1,0:T(2,128)(2,1)} %all_to_all.119), calls=%async_computation.5 | async-start | bytes 8192 | tf_op jit(solution)/shard_map/all_to_all | solution.py:116
  149.7 2.1 collective-permute-start.2
  168.2 8.6 %all-to-all-start.6 = ((bf16[4,2,128]{2,1,0:T(2,128)(2,1)}), bf16[4,2,128]{2,1,0:T(2,128)(2,1)S(1)}, u32[]{:S(2)}, u32[]{:S(2)}) async-start(bf16[4,2,128]{2,1,0:T(2,128)(2,1)} %bitcast.46), calls=%async_computation.6 | async-start | bytes 4096 | tf_op jit(solution)/shard_map/all_to_all | solution.py:115
  176.9 8.8 %all-to-all-start.7 = ((bf16[4,2,256]{2,1,0:T(2,128)(2,1)}), bf16[4,2,256]{2,1,0:T(2,128)(2,1)S(1)}, u32[]{:S(2)}, u32[]{:S(2)}) async-start(bf16[4,2,256]{2,1,0:T(2,128)(2,1)} %all_to_all.125), calls=%async_computation.7 | async-start | bytes 8192 | tf_op jit(solution)/shard_map/all_to_all | solution.py:116
where the time goes:
time: 217 us; the launch traced here: 216 us
  blocking collectives  118 us (54%)
  starting transfers between devices  32.4 us (15%)
  waiting for transfers between devices  31.4 us (14%)
  matrix products  21.6 us (10%)
  other arithmetic  7.26 us (3%)
  local copies, waits for them, and re-layouts  5.14 us (2%)
    all_gather x4, blocking collectives, shards(): whole = lax.all_gather(carried, 'tensor', axis=1, tiled=True)  55.7 us
    all_gather x4, blocking collectives, shards(): lax.all_gather(mixture, 'tensor', axis=0, tiled=True)  47.7 us
    all_to_all x4, waiting for transfers between devices, shards(): lax.all_to_all(fresh_kv, 'tensor', split_axis=0, concat_axis=1, tiled=True)  22.2 us
    all_to_all x1, blocking collectives, shards(): lax.all_to_all(outgoing, 'section', split_axis=1, concat_axis=0, tiled=True)  14.9 us
    all_to_all x4, starting transfers between devices, shards(): lax.all_to_all(queries, 'tensor', split_axis=0, concat_axis=1, tiled=True)  14.4 us
    all_to_all x4, starting transfers between devices, shards(): lax.all_to_all(fresh_kv, 'tensor', split_axis=0, concat_axis=1, tiled=True)  13.8 us
    dot_general x4, matrix products, shards(): jnp.dot(normed, kv_proj, preferred_element_type=jnp.float32)  11.5 us
    dot_general x4, matrix products, shards(): jnp.dot(normed, query_proj, preferred_element_type=jnp.float32) + bias_row  7.34 us
  transfers between devices with their start and end apart: 11, of which 11 were waited for; matrix products, arithmetic and copies ran while one was open for 6% of the time, Pallas kernels for 0%

commit v1 on v0

--- a/solution.py
+++ b/solution.py
@@ -1,6 +1,10 @@
+import functools
+
 import jax
 import jax.numpy as jnp
 from jax import lax
+from jax.experimental import pallas as pl
+from jax.experimental.pallas import tpu as pltpu
 from jax.sharding import PartitionSpec as P
 
 HD = 128
@@ -145,9 +149,415 @@
     return spread[section_count - 1]
 
 
+MESH = pl.DeviceIdType.MESH
+ANY = pl.BlockSpec(memory_space=pl.ANY)
+VMEM = pl.BlockSpec(memory_space=pltpu.VMEM)
+SMEM = pl.BlockSpec(memory_space=pltpu.SMEM)
+
+
+def fused(
+    slots,
+    sections,
+    hidden,
+    gain,
+    wq,
+    bias,
+    wkv,
+    wo,
+    pool,
+    table,
+    lens,
+    out,
+    wq_v,
+    wkv_v,
+    wo_v,
+    stream,
+    keys,
+    values,
+    meta,
+    counts,
+    cos_v,
+    sin_v,
+    fresh,
+    parts,
+    sent,
+    fin,
+    fin_in,
+    w_sem,
+    pool_sem,
+    st_send,
+    st_recv,
+    nx_send,
+    key_send,
+    key_recv,
+    val_send,
+    val_recv,
+    meta_send,
+    meta_recv,
+    fresh_send,
+    fresh_recv,
+    part_send,
+    part_recv,
+    fin_send,
+    fin_recv,
+):
+    f32, bf16 = jnp.float32, jnp.bfloat16
+    me = lax.axis_index("tensor")
+    sec = lax.axis_index("section")
+    rows, width = hidden.shape
+    row_dev, blocks = table.shape
+    pages, page_len = pool.shape[1], pool.shape[2]
+    span = pages * page_len
+    span_pad = keys.shape[1] * page_len
+    kv_cols = wkv.shape[2]
+    kv_half = KVH * HD
+    group = slots // KVH
+    near = sorted(range(slots), key=lambda d: min(d, slots - d))
+    others = near[1:]
+    far = near[::-1]
+
+    def peer(d):
+        return lax.rem(me + d, slots)
+
+    def chunk(ref, src):
+        return ref.at[pl.ds(pl.multiple_of(src * width, width), width)]
+
+    def weight_copies(src):
+        return (
+            pltpu.make_async_copy(chunk(wq.at[0], src), chunk(wq_v, src), w_sem.at[0, src]),
+            pltpu.make_async_copy(chunk(wkv.at[0], src), chunk(wkv_v, src), w_sem.at[1, src]),
+        )
+
+    def remote(src, dst, send, recv, slot, section):
+        return pltpu.make_async_remote_copy(
+            src_ref=src,
+            dst_ref=dst,
+            send_sem=send,
+            recv_sem=recv,
+            device_id={"tensor": slot, "section": section},
+            device_id_type=MESH,
+        )
+
+    for d in near:
+        for copy in weight_copies(peer(d)):
+            copy.start()
+    wo_copy = pltpu.make_async_copy(wo.at[0], wo_v, w_sem.at[2, 0])
+    wo_copy.start()
+
+    barrier = pltpu.get_barrier_semaphore()
+    for d in range(slots):
+        for e in range(sections):
+            if d or e:
+                pl.semaphore_signal(
+                    barrier,
+                    inc=1,
+                    device_id={"tensor": peer(d), "section": lax.rem(sec + e, sections)},
+                    device_id_type=MESH,
+                )
+
+    lane = lax.broadcasted_iota(jnp.int32, (row_dev, span_pad), 1)
+    row = lax.broadcasted_iota(jnp.int32, (row_dev, span_pad), 0)
+    row_c = lax.broadcasted_iota(jnp.int32, (row_dev, HD), 0)
+    count = jnp.zeros((row_dev, span_pad), f32)
+    length = jnp.zeros((row_dev, HD), f32)
+    for r in range(row_dev):
+        for b in range(blocks):
+            off = lane - (table[r, b] - me * pages) * page_len
+            used = (off >= 0) & (off < page_len) & (off + b * page_len < lens[r]) & (row == r)
+            count += jnp.where(used, 1.0, 0.0)
+        length = jnp.where(row_c == r, lens[r].astype(f32), length)
+    meta[me, :, :span_pad] = count
+    meta[me, :, span_pad:] = length
+    for ref in (keys, values):
+        if span_pad > span:
+            ref[:, pages:] = jnp.zeros((slots, span_pad // page_len - pages, page_len, HD), bf16)
+
+    pl.semaphore_wait(barrier, slots * sections - 1)
+
+    @pl.when(sec == 0)
+    def _():
+        for d in far[:-1]:
+            remote(hidden, stream.at[me], st_send.at[d], st_recv.at[me], peer(d), sec).start()
+        stream[me] = hidden[...]
+
+    def pool_part(slot, base):
+        first = pl.multiple_of(base + (slot // group) * HD, HD)
+        return pool.at[0, :, :, pl.ds(first, HD)]
+
+    meta_copies, pool_copies = [], []
+    for d in others:
+        slot = peer(d)
+        meta_copies.append(
+            remote(meta.at[me], meta.at[me], meta_send.at[d], meta_recv.at[me], slot, sec)
+        )
+        pool_copies.append(
+            remote(
+                pool_part(slot, 0),
+                keys.at[me, pl.ds(0, pages)],
+                key_send.at[d],
+                key_recv.at[me],
+                slot,
+                sec,
+            )
+        )
+        pool_copies.append(
+            remote(
+                pool_part(slot, kv_half),
+                values.at[me, pl.ds(0, pages)],
+                val_send.at[d],
+                val_recv.at[me],
+                slot,
+                sec,
+            )
+        )
+    own_pool = [
+        pltpu.make_async_copy(pool_part(me, 0), keys.at[me, pl.ds(0, pages)], pool_sem.at[0]),
+        pltpu.make_async_copy(
+            pool_part(me, kv_half), values.at[me, pl.ds(0, pages)], pool_sem.at[1]
+        ),
+    ]
+    for copy in meta_copies + pool_copies + own_pool:
+        copy.start()
+
+    def arrived(dst, recv):
+        remote(dst, dst, fin_send.at[0], recv, me, lax.rem(sec + 1, sections)).wait_recv()
+
+    for d in others:
+        src = peer(d)
+        arrived(meta.at[src], meta_recv.at[src])
+    counts[...] = jnp.zeros(counts.shape, f32)
+    for t in range(slots):
+        lines = slice(t * row_dev, (t + 1) * row_dev)
+        counts[lines, t * span_pad : (t + 1) * span_pad] = meta[t, :, :span_pad]
+        cos_v[lines, :] = meta[t, :, span_pad:]
+    spot = lax.broadcasted_iota(jnp.int32, (rows, HD), 1)
+    half = HD // 2
+    pair = jnp.where(spot < half, spot, spot - half).astype(f32)
+    frequency = jnp.exp(pair * (-2.0 / HD) * jnp.log(jnp.full((rows, HD), rope_base, f32)))
+    angle = cos_v[...] * frequency
+    cosine = jnp.cos(angle)
+    sine = jnp.sin(angle) * jnp.where(spot < half, -1.0, 1.0)
+    cos_v[...] = cosine
+    sin_v[...] = sine
+
+    def rope(x):
+        x = x.astype(f32)
+        return (x * cos_v[...] + pltpu.roll(x, half, 1) * sin_v[...]).astype(bf16)
+
+    square = jnp.zeros((rows, 1), f32)
+    q_sum = jnp.zeros((rows, HD), f32)
+    kv_sum = jnp.zeros((rows, kv_cols), f32)
+    for d in near:
+        src = peer(d)
+        for copy in weight_copies(src):
+            copy.wait()
+        if d == 0:
+
+            @pl.when(sec > 0)
+            def _():
+                arrived(stream.at[me], st_recv.at[me])
+
+        else:
+            arrived(stream.at[src], st_recv.at[src])
+        start = pl.multiple_of(src * width, width)
+        x = stream[src].astype(f32)
+        square += jnp.sum(x * x, axis=1, keepdims=True)
+        scaled = (x * gain[:, pl.ds(start, width)].astype(f32)).astype(bf16)
+        q_sum += jnp.dot(scaled, wq_v[pl.ds(start, width), :], preferred_element_type=f32)
+        kv_sum += jnp.dot(scaled, wkv_v[pl.ds(start, width), :], preferred_element_type=f32)
+    inverse = lax.rsqrt(square * (1.0 / (slots * width)) + epsilon)
+    query = rope((q_sum * inverse + bias[...].astype(f32)).astype(bf16))
+    kv_new = (kv_sum * inverse).astype(bf16)
+    fresh[me, :, :HD] = query
+    for j in range(kv_cols // HD):
+        piece = kv_new[:, j * HD : (j + 1) * HD]
+        is_key = me * kv_cols + j * HD < kv_half
+        fresh[me, :, (j + 1) * HD : (j + 2) * HD] = jnp.where(
+            is_key, rope(piece).astype(f32), piece.astype(f32)
+        ).astype(bf16)
+    fresh_copies = [
+        remote(fresh.at[me], fresh.at[me], fresh_send.at[d], fresh_recv.at[me], peer(d), sec)
+        for d in far[:-1]
+    ]
+    for copy in fresh_copies:
+        copy.start()
+
+    for copy in own_pool:
+        copy.wait()
+    for d in others:
+        src = peer(d)
+        arrived(keys.at[src, pl.ds(0, pages)], key_recv.at[src])
+        arrived(values.at[src, pl.ds(0, pages)], val_recv.at[src])
+    scaling = HD**-0.5
+    times = counts[...]
+    scores = (
+        lax.dot_general(
+            query,
+            keys[...].reshape(slots * span_pad, HD),
+            (((1,), (1,)), ((), ())),
+            preferred_element_type=f32,
+        )
+        * scaling
+    )
+    top = jnp.max(jnp.where(times > 0, scores, -1e30), axis=1, keepdims=True)
+    weights = jnp.where(times > 0, times * jnp.exp(scores - top), 0.0)
+    total = jnp.sum(weights, axis=1, keepdims=True)
+    mixed = jnp.dot(
+        weights.astype(bf16),
+        values[...].reshape(slots * span_pad, HD),
+        preferred_element_type=f32,
+    )
+    parts[me, :, :HD] = mixed / total
+    parts[me, :, HD:] = jnp.broadcast_to(top + jnp.log(total), (rows, HD))
+    part_copies = [
+        remote(parts.at[me], parts.at[me], part_send.at[d], part_recv.at[me], peer(d), sec)
+        for d in far[:-1]
+    ]
+    for copy in part_copies:
+        copy.start()
+
+    for d in others:
+        src = peer(d)
+        arrived(fresh.at[src], fresh_recv.at[src])
+
+    def fresh_head(column):
+        first = HD + column % kv_cols
+        return fresh[column // kv_cols, :, first : first + HD].astype(f32)
+
+    own = []
+    for h in range(slots):
+        key = fresh_head((h // group) * HD)
+        own.append(
+            jnp.sum(fresh[h, :, :HD].astype(f32) * key, axis=1, keepdims=True) * scaling
+        )
+    wo_copy.wait()
+    for d in others:
+        src = peer(d)
+        arrived(parts.at[src], part_recv.at[src])
+    mixture = []
+    for h in range(slots):
+        share = 1.0 / (1.0 + jnp.exp(parts[h, :, HD:] - own[h]))
+        value = fresh_head(kv_half + (h // group) * HD)
+        mixture.append((parts[h, :, :HD] * (1.0 - share) + value * share).astype(bf16))
+    mixture = jnp.concatenate(mixture, axis=1)
+    new = (
+        stream[me].astype(f32) + jnp.dot(mixture, wo_v[...], preferred_element_type=f32)
+    ).astype(bf16)
+
+    def next_copies():
+        return [
+            remote(sent, stream.at[me], nx_send.at[d], st_recv.at[me], peer(d), sec + 1)
+            for d in far
+        ]
+
+    def fin_copy(j):
+        return remote(fin.at[j], fin_in, fin_send.at[j], fin_recv, me, j)
+
+    last = sections - 1
+
+    @pl.when(sec < last)
+    def _():
+        sent[...] = new
+        for copy in next_copies():
+            copy.start()
+        arrived(fin_in, fin_recv)
+        out[...] = fin_in[...]
+        for copy in next_copies():
+            copy.wait_send()
+
+    @pl.when(sec == last)
+    def _():
+        out_rows = rows // sections
+        wide = new.astype(f32)
+        for j in range(last):
+            fin[j] = wide[j * out_rows : (j + 1) * out_rows].astype(bf16)
+            fin_copy(j).start()
+        out[...] = wide[last * out_rows :].astype(bf16)
+        for j in range(last):
+            fin_copy(j).wait_send()
+
+    @pl.when(sec == 0)
+    def _():
+        for d in others:
+            remote(hidden, stream.at[me], st_send.at[d], st_recv.at[me], peer(d), sec).wait_send()
+
+    for copy in meta_copies + pool_copies + fresh_copies + part_copies:
+        copy.wait_send()
+
+
+def fused_shards(slots, sections, *args):
+    hidden, gain, wq, bias, wkv, wo, pool, table, lens = args
+    rows, width = hidden.shape
+    row_dev = table.shape[0]
+    pages, page_len = pool.shape[1:3]
+    span_pad = -(-pages * page_len // HD) * HD
+    pages_pad = span_pad // page_len
+    kv_cols = wkv.shape[2]
+    bf16, f32 = jnp.bfloat16, jnp.float32
+    dma = pltpu.SemaphoreType.DMA
+    each = dma((slots,))
+    return pl.pallas_call(
+        functools.partial(fused, slots, sections),
+        out_shape=jax.ShapeDtypeStruct((rows // sections, width), bf16),
+        in_specs=[VMEM, VMEM, ANY, VMEM, ANY, ANY, ANY, SMEM, SMEM],
+        out_specs=VMEM,
+        scratch_shapes=[
+            pltpu.VMEM(wq.shape[1:], bf16),
+            pltpu.VMEM(wkv.shape[1:], bf16),
+            pltpu.VMEM(wo.shape[1:], bf16),
+            pltpu.VMEM((slots, rows, width), bf16),
+            pltpu.VMEM((slots, pages_pad, page_len, HD), bf16),
+            pltpu.VMEM((slots, pages_pad, page_len, HD), bf16),
+            pltpu.VMEM((slots, row_dev, span_pad + HD), f32),
+            pltpu.VMEM((rows, slots * span_pad), f32),
+            pltpu.VMEM((rows, HD), f32),
+            pltpu.VMEM((rows, HD), f32),
+            pltpu.VMEM((slots, rows, HD + kv_cols), bf16),
+            pltpu.VMEM((slots, rows, 2 * HD), f32),
+            pltpu.VMEM((rows, width), bf16),
+            pltpu.VMEM((sections, rows // sections, width), bf16),
+            pltpu.VMEM((rows // sections, width), bf16),
+            dma((3, slots)),
+            dma((2,)),
+            each,
+            each,
+            each,
+            each,
+            each,
+            each,
+            each,
+            each,
+            each,
+            each,
+            each,
+            each,
+            each,
+            dma((sections,)),
+            dma,
+        ],
+        compiler_params=pltpu.CompilerParams(
+            collective_id=0, has_side_effects=True, vmem_limit_bytes=56 * 1024 * 1024
+        ),
+        name="decode_stack",
+    )(*args)
+
+
+def pick(slots, sections, *args):
+    hidden, gain, wq, bias, wkv = args[:5]
+    fits = (
+        wq.shape[2] == HD
+        and wkv.shape[2] % HD == 0
+        and slots % KVH == 0
+        and sections > 1
+        and slots > 1
+        and hidden.shape[0] % sections == 0
+    )
+    return fused_shards(slots, sections, *args) if fits else shards(*args)
+
+
 def solution(mesh):
     return jax.shard_map(
-        shards,
+        functools.partial(pick, mesh.shape["tensor"], mesh.shape["section"]),
         mesh=mesh,
         in_specs=(
             P("groups", "tensor"),

time: 217 us -> 53 us (0.24)
  blocking collectives: 118 us -> 0 us
  Pallas kernels: 0 us -> 51.5 us
  starting transfers between devices: 32.4 us -> 0 us
  waiting for transfers between devices: 31.4 us -> 0 us
  matrix products: 21.6 us -> 0 us
  other arithmetic: 7.26 us -> 0 us
  local copies, waits for them, and re-layouts: 5.14 us -> 1.3 us
    all_gather x8 -> x0, blocking collectives: 103 us -> none  [the longest x4 55.7 us: shards(): whole = lax.all_gather(carried, 'tensor', axis=1, tiled=True)]
    pallas_call x0 -> x1, Pallas kernels: none -> 51.5 us  [fused_shards(): pl.pallas_call(functools.partial(fused, slots, sections), out_shape=jax.S...]
    all_to_all x8 -> x0, waiting for transfers between devices: 28.9 us -> none  [the longest x4 22.2 us: shards(): lax.all_to_all(fresh_kv, 'tensor', split_axis=0, concat_axis=1, tiled=True)]
    all_to_all x8 -> x0, starting transfers between devices: 28.2 us -> none  [the longest x4 14.4 us: shards(): lax.all_to_all(queries, 'tensor', split_axis=0, concat_axis=1, tiled=True)]
    dot_general x20 -> x0, matrix products: 21.6 us -> none  [the longest x4 11.5 us: shards(): jnp.dot(normed, kv_proj, preferred_element_type=jnp.float32)]
    all_to_all x1 -> x0, blocking collectives: 14.9 us -> none  [shards(): lax.all_to_all(outgoing, 'section', split_axis=1, concat_axis=0, tiled=True)]
    ppermute x3 -> x0, starting transfers between devices: 4.12 us -> none  [shifted(): lax.ppermute(value, axis, [(source, source + steps) for source in range(i...]
    all_to_all x6 -> x0, local copies, waits for them, and re-layouts: 2.66 us -> none  [the longest x4 2.45 us: shards(): lax.all_to_all(fresh_kv, 'tensor', split_axis=0, concat_axis=1, tiled=True)]
  transfers between devices with their start and end apart: 11 -> 0, of which waited for: 11 -> 0; matrix products, arithmetic and copies ran while one was open for 6% -> 0% of each run, Pallas kernels for 0% -> 0%
where the time goes in v1:
time: 53 us; the launch traced here: 52.8 us
  Pallas kernels  51.5 us (97%)
  local copies, waits for them, and re-layouts  1.3 us (2%)
    pallas_call x1, Pallas kernels, fused_shards(): pl.pallas_call(functools.partial(fused, slots, sections), out_shape=jax.S...  51.5 us
    unnamed x1, local copies, waits for them, and re-layouts  1.3 us

profile of v1, /device:TPU:0, one launch (start us, length us, event | category | flops | bytes accessed | tf_op | source)
XLA Modules:
  0.0 52.8 jit_solution(15963026746931023661)
XLA Ops:
  0.0 51.5 %decode_stack.1 = bf16[2,2048]{1,0:T(2,128)(2,1)} custom-call(bf16[8,2048]{1,0:T(8,128)(2,1)} %hidden.1, bf16[1,8192]{1,0:T(2,128)(2,1)} %gain.1, bf16[1,8192,128]{2,1,0:T(8,128)(2,1)} %wq.1, bf16[1,128]{1,0:T(2,128)(2,1)} %bias.1, bf16[1,8192,256]{2,1,0:T(8,128)(2,1)} %wkv.1, bf16[1,512,2048]{2,1,0:T(8,128)(2,1)} %wo.1, bf16[1,6,16,1024]{3,2,1,0:T(8,128)(2,1)} %pool.1, ...), custom_call_target="tpu_custom_call" | custom-call | tf_op jit(solution)/shard_map/decode_stack/pallas_call | solution.py:499
  51.5 1.3 %copy.11 = bf16[2,2048]{1,0:T(2,128)(2,1)} copy(bf16[2,2048]{1,0:T(2,128)(2,1)} %decode_stack.1) | data formatting | bytes 16384

commit v2 on v1

--- a/solution.py
+++ b/solution.py
@@ -152,22 +152,26 @@
 MESH = pl.DeviceIdType.MESH
 ANY = pl.BlockSpec(memory_space=pl.ANY)
 VMEM = pl.BlockSpec(memory_space=pltpu.VMEM)
-SMEM = pl.BlockSpec(memory_space=pltpu.SMEM)
 
 
 def fused(
     slots,
     sections,
     hidden,
-    gain,
+    gain_in,
     wq,
-    bias,
+    bias_in,
     wkv,
     wo,
+    pool_in,
+    table_in,
+    lens_in,
+    out,
+    gain,
+    bias,
     pool,
     table,
     lens,
-    out,
     wq_v,
     wkv_v,
     wo_v,
@@ -200,24 +204,53 @@
     part_recv,
     fin_send,
     fin_recv,
+    small_sem,
+    go_sem,
 ):
     f32, bf16 = jnp.float32, jnp.bfloat16
     me = lax.axis_index("tensor")
     sec = lax.axis_index("section")
     rows, width = hidden.shape
     row_dev, blocks = table.shape
-    pages, page_len = pool.shape[1], pool.shape[2]
+    pages, page_len = pool.shape[:2]
     span = pages * page_len
     span_pad = keys.shape[1] * page_len
     kv_cols = wkv.shape[2]
     kv_half = KVH * HD
     group = slots // KVH
-    near = sorted(range(slots), key=lambda d: min(d, slots - d))
-    others = near[1:]
-    far = near[::-1]
-
-    def peer(d):
-        return lax.rem(me + d, slots)
+    last = sections - 1
+    others = range(1, slots)
+
+    ranked = [sorted(range(slots), key=lambda t: abs(t - m)) for m in range(slots)]
+    near = [
+        sum((me == m).astype(jnp.int32) * ranked[m][k] for m in range(slots))
+        for k in range(slots)
+    ]
+
+    def peer(k):
+        return near[k]
+
+    barrier = pltpu.get_barrier_semaphore()
+
+    def greet(slot, section):
+        pl.semaphore_signal(
+            barrier,
+            inc=1,
+            device_id={"tensor": slot, "section": section},
+            device_id_type=MESH,
+        )
+
+    for k in others:
+        greet(peer(k), sec)
+
+    @pl.when(sec > 0)
+    def _():
+        for t in range(slots):
+            greet(t, sec - 1)
+
+    @pl.when(sec < last)
+    def _():
+        greet(me, last)
 
     def chunk(ref, src):
         return ref.at[pl.ds(pl.multiple_of(src * width, width), width)]
@@ -238,23 +271,27 @@
             device_id_type=MESH,
         )
 
-    for d in near:
-        for copy in weight_copies(peer(d)):
+    hidden_copy = pltpu.make_async_copy(hidden, stream.at[me], small_sem.at[0])
+    table_copy = pltpu.make_async_copy(table_in, table, small_sem.at[1])
+    lens_copy = pltpu.make_async_copy(lens_in, lens, small_sem.at[2])
+    gain_copy = pltpu.make_async_copy(gain_in, gain, small_sem.at[3])
+    bias_copy = pltpu.make_async_copy(bias_in, bias, small_sem.at[4])
+    pool_copy = pltpu.make_async_copy(pool_in.at[0], pool, small_sem.at[5])
+
+    @pl.when(sec == 0)
+    def _():
+        hidden_copy.start()
+
+    for copy in (table_copy, lens_copy, pool_copy, gain_copy, bias_copy):
+        copy.start()
+    for k in range(slots):
+        for copy in weight_copies(peer(k)):
             copy.start()
     wo_copy = pltpu.make_async_copy(wo.at[0], wo_v, w_sem.at[2, 0])
     wo_copy.start()
 
-    barrier = pltpu.get_barrier_semaphore()
-    for d in range(slots):
-        for e in range(sections):
-            if d or e:
-                pl.semaphore_signal(
-                    barrier,
-                    inc=1,
-                    device_id={"tensor": peer(d), "section": lax.rem(sec + e, sections)},
-                    device_id_type=MESH,
-                )
-
+    table_copy.wait()
+    lens_copy.wait()
     lane = lax.broadcasted_iota(jnp.int32, (row_dev, span_pad), 1)
     row = lax.broadcasted_iota(jnp.int32, (row_dev, span_pad), 0)
     row_c = lax.broadcasted_iota(jnp.int32, (row_dev, HD), 0)
@@ -272,17 +309,23 @@
         if span_pad > span:
             ref[:, pages:] = jnp.zeros((slots, span_pad // page_len - pages, page_len, HD), bf16)
 
-    pl.semaphore_wait(barrier, slots * sections - 1)
+    pl.semaphore_wait(barrier, 2 * slots - 1 + (last - slots) * (sec // last))
+
+    def first_copies():
+        return [
+            remote(stream.at[me], stream.at[me], st_send.at[d], st_recv.at[me], peer(d), sec)
+            for d in reversed(others)
+        ]
 
     @pl.when(sec == 0)
     def _():
-        for d in far[:-1]:
-            remote(hidden, stream.at[me], st_send.at[d], st_recv.at[me], peer(d), sec).start()
-        stream[me] = hidden[...]
+        hidden_copy.wait()
+        for copy in first_copies():
+            copy.start()
 
     def pool_part(slot, base):
         first = pl.multiple_of(base + (slot // group) * HD, HD)
-        return pool.at[0, :, :, pl.ds(first, HD)]
+        return pool.at[:, :, pl.ds(first, HD)]
 
     meta_copies, pool_copies = [], []
     for d in others:
@@ -316,7 +359,20 @@
             pool_part(me, kv_half), values.at[me, pl.ds(0, pages)], pool_sem.at[1]
         ),
     ]
-    for copy in meta_copies + pool_copies + own_pool:
+    for copy in meta_copies:
+        copy.start()
+
+    @pl.when(sec == 0)
+    def _():
+        for copy in first_copies():
+            copy.wait_send()
+
+    @pl.when(sec > 0)
+    def _():
+        pl.semaphore_wait(go_sem, 1)
+
+    pool_copy.wait()
+    for copy in pool_copies + own_pool:
         copy.start()
 
     def arrived(dst, recv):
@@ -347,7 +403,9 @@
     square = jnp.zeros((rows, 1), f32)
     q_sum = jnp.zeros((rows, HD), f32)
     kv_sum = jnp.zeros((rows, kv_cols), f32)
-    for d in near:
+    gain_copy.wait()
+    bias_copy.wait()
+    for d in range(slots):
         src = peer(d)
         for copy in weight_copies(src):
             copy.wait()
@@ -377,7 +435,7 @@
         ).astype(bf16)
     fresh_copies = [
         remote(fresh.at[me], fresh.at[me], fresh_send.at[d], fresh_recv.at[me], peer(d), sec)
-        for d in far[:-1]
+        for d in reversed(others)
     ]
     for copy in fresh_copies:
         copy.start()
@@ -388,6 +446,13 @@
         src = peer(d)
         arrived(keys.at[src, pl.ds(0, pages)], key_recv.at[src])
         arrived(values.at[src, pl.ds(0, pages)], val_recv.at[src])
+
+    @pl.when(sec < last)
+    def _():
+        pl.semaphore_signal(
+            go_sem, inc=1, device_id={"tensor": me, "section": sec + 1}, device_id_type=MESH
+        )
+
     scaling = HD**-0.5
     times = counts[...]
     scores = (
@@ -411,7 +476,7 @@
     parts[me, :, HD:] = jnp.broadcast_to(top + jnp.log(total), (rows, HD))
     part_copies = [
         remote(parts.at[me], parts.at[me], part_send.at[d], part_recv.at[me], peer(d), sec)
-        for d in far[:-1]
+        for d in reversed(others)
     ]
     for copy in part_copies:
         copy.start()
@@ -421,39 +486,37 @@
         arrived(fresh.at[src], fresh_recv.at[src])
 
     def fresh_head(column):
-        first = HD + column % kv_cols
-        return fresh[column // kv_cols, :, first : first + HD].astype(f32)
-
-    own = []
-    for h in range(slots):
+        first = pl.multiple_of(HD + lax.rem(column, kv_cols), HD)
+        return fresh[column // kv_cols, :, pl.ds(first, HD)].astype(f32)
+
+    own, fresh_values = [], []
+    for k in range(slots):
+        h = peer(k)
         key = fresh_head((h // group) * HD)
         own.append(
             jnp.sum(fresh[h, :, :HD].astype(f32) * key, axis=1, keepdims=True) * scaling
         )
+        fresh_values.append(fresh_head(kv_half + (h // group) * HD))
     wo_copy.wait()
-    for d in others:
-        src = peer(d)
-        arrived(parts.at[src], part_recv.at[src])
-    mixture = []
-    for h in range(slots):
-        share = 1.0 / (1.0 + jnp.exp(parts[h, :, HD:] - own[h]))
-        value = fresh_head(kv_half + (h // group) * HD)
-        mixture.append((parts[h, :, :HD] * (1.0 - share) + value * share).astype(bf16))
-    mixture = jnp.concatenate(mixture, axis=1)
-    new = (
-        stream[me].astype(f32) + jnp.dot(mixture, wo_v[...], preferred_element_type=f32)
-    ).astype(bf16)
+    summed = stream[me].astype(f32)
+    for k in range(slots):
+        h = peer(k)
+        if k:
+            arrived(parts.at[h], part_recv.at[h])
+        share = 1.0 / (1.0 + jnp.exp(parts[h, :, HD:] - own[k]))
+        mixture = (parts[h, :, :HD] * (1.0 - share) + fresh_values[k] * share).astype(bf16)
+        lines = pl.ds(pl.multiple_of(h * HD, HD), HD)
+        summed += jnp.dot(mixture, wo_v[lines, :], preferred_element_type=f32)
+    new = summed.astype(bf16)
 
     def next_copies():
         return [
             remote(sent, stream.at[me], nx_send.at[d], st_recv.at[me], peer(d), sec + 1)
-            for d in far
+            for d in reversed(range(slots))
         ]
 
     def fin_copy(j):
         return remote(fin.at[j], fin_in, fin_send.at[j], fin_recv, me, j)
-
-    last = sections - 1
 
     @pl.when(sec < last)
     def _():
@@ -475,11 +538,6 @@
         out[...] = wide[last * out_rows :].astype(bf16)
         for j in range(last):
             fin_copy(j).wait_send()
-
-    @pl.when(sec == 0)
-    def _():
-        for d in others:
-            remote(hidden, stream.at[me], st_send.at[d], st_recv.at[me], peer(d), sec).wait_send()
 
     for copy in meta_copies + pool_copies + fresh_copies + part_copies:
         copy.wait_send()
@@ -499,9 +557,14 @@
     return pl.pallas_call(
         functools.partial(fused, slots, sections),
         out_shape=jax.ShapeDtypeStruct((rows // sections, width), bf16),
-        in_specs=[VMEM, VMEM, ANY, VMEM, ANY, ANY, ANY, SMEM, SMEM],
+        in_specs=[ANY] * 9,
         out_specs=VMEM,
         scratch_shapes=[
+            pltpu.VMEM(gain.shape, bf16),
+            pltpu.VMEM(bias.shape, bf16),
+            pltpu.VMEM(pool.shape[1:], bf16),
+            pltpu.SMEM(table.shape, jnp.int32),
+            pltpu.SMEM(lens.shape, jnp.int32),
             pltpu.VMEM(wq.shape[1:], bf16),
             pltpu.VMEM(wkv.shape[1:], bf16),
             pltpu.VMEM(wo.shape[1:], bf16),
@@ -534,6 +597,8 @@
             each,
             dma((sections,)),
             dma,
+            dma((6,)),
+            pltpu.SemaphoreType.REGULAR,
         ],
         compiler_params=pltpu.CompilerParams(
             collective_id=0, has_side_effects=True, vmem_limit_bytes=56 * 1024 * 1024

time: 53 us -> 46.3 us (0.87)
  Pallas kernels: 51.5 us -> 44.8 us
    pallas_call x1, Pallas kernels: 51.5 us -> 44.8 us  [fused_shards(): pl.pallas_call(functools.partial(fused, slots, sections), out_shape=jax.S...]
where the time goes in v2:
time: 46.3 us; the launch traced here: 46.1 us
  Pallas kernels  44.8 us (97%)
  local copies, waits for them, and re-layouts  1.3 us (3%)
    pallas_call x1, Pallas kernels, fused_shards(): pl.pallas_call(functools.partial(fused, slots, sections), out_shape=jax.S...  44.8 us
    unnamed x1, local copies, waits for them, and re-layouts  1.3 us

profile of v2, /device:TPU:0, one launch (start us, length us, event | category | flops | bytes accessed | tf_op | source)
XLA Modules:
  0.0 46.1 jit_solution(3968680407950363062)
XLA Ops:
  0.0 44.8 %decode_stack.1 = bf16[2,2048]{1,0:T(2,128)(2,1)} custom-call(bf16[8,2048]{1,0:T(8,128)(2,1)} %hidden.1, bf16[1,8192]{1,0:T(2,128)(2,1)} %gain_in.1, bf16[1,8192,128]{2,1,0:T(8,128)(2,1)} %wq.1, bf16[1,128]{1,0:T(2,128)(2,1)} %bias_in.1, bf16[1,8192,256]{2,1,0:T(8,128)(2,1)} %wkv.1, bf16[1,512,2048]{2,1,0:T(8,128)(2,1)} %wo.1, ...), custom_call_target="tpu_custom_call" | custom-call | tf_op jit(solution)/shard_map/decode_stack/pallas_call | solution.py:557
  44.8 1.3 %copy.11 = bf16[2,2048]{1,0:T(2,128)(2,1)} copy(bf16[2,2048]{1,0:T(2,128)(2,1)} %decode_stack.1) | data formatting | bytes 16384

commit v3 on v2

--- a/solution.py
+++ b/solution.py
@@ -150,7 +150,7 @@
 
 
 MESH = pl.DeviceIdType.MESH
-ANY = pl.BlockSpec(memory_space=pl.ANY)
+HBM = pl.BlockSpec(memory_space=pltpu.HBM)
 VMEM = pl.BlockSpec(memory_space=pltpu.VMEM)
 
 
@@ -221,7 +221,9 @@
     last = sections - 1
     others = range(1, slots)
 
-    ranked = [sorted(range(slots), key=lambda t: abs(t - m)) for m in range(slots)]
+    ranked = [
+        sorted(range(slots), key=lambda t: (abs(t - m), t // 2 != m // 2)) for m in range(slots)
+    ]
     near = [
         sum((me == m).astype(jnp.int32) * ranked[m][k] for m in range(slots))
         for k in range(slots)
@@ -289,6 +291,20 @@
             copy.start()
     wo_copy = pltpu.make_async_copy(wo.at[0], wo_v, w_sem.at[2, 0])
     wo_copy.start()
+
+    pl.semaphore_wait(barrier, 2 * slots - 1 + (last - slots) * (sec // last))
+
+    def first_copies():
+        return [
+            remote(stream.at[me], stream.at[me], st_send.at[d], st_recv.at[me], peer(d), sec)
+            for d in reversed(others)
+        ]
+
+    @pl.when(sec == 0)
+    def _():
+        hidden_copy.wait()
+        for copy in first_copies():
+            copy.start()
 
     table_copy.wait()
     lens_copy.wait()
@@ -305,29 +321,16 @@
         length = jnp.where(row_c == r, lens[r].astype(f32), length)
     meta[me, :, :span_pad] = count
     meta[me, :, span_pad:] = length
+
     for ref in (keys, values):
         if span_pad > span:
             ref[:, pages:] = jnp.zeros((slots, span_pad // page_len - pages, page_len, HD), bf16)
 
-    pl.semaphore_wait(barrier, 2 * slots - 1 + (last - slots) * (sec // last))
-
-    def first_copies():
-        return [
-            remote(stream.at[me], stream.at[me], st_send.at[d], st_recv.at[me], peer(d), sec)
-            for d in reversed(others)
-        ]
-
-    @pl.when(sec == 0)
-    def _():
-        hidden_copy.wait()
-        for copy in first_copies():
-            copy.start()
-
     def pool_part(slot, base):
         first = pl.multiple_of(base + (slot // group) * HD, HD)
         return pool.at[:, :, pl.ds(first, HD)]
 
-    meta_copies, pool_copies = [], []
+    meta_copies, pool_copies, value_copies = [], [], []
     for d in others:
         slot = peer(d)
         meta_copies.append(
@@ -343,7 +346,7 @@
                 sec,
             )
         )
-        pool_copies.append(
+        value_copies.append(
             remote(
                 pool_part(slot, kv_half),
                 values.at[me, pl.ds(0, pages)],
@@ -362,39 +365,39 @@
     for copy in meta_copies:
         copy.start()
 
-    @pl.when(sec == 0)
-    def _():
-        for copy in first_copies():
-            copy.wait_send()
-
-    @pl.when(sec > 0)
+    @pl.when(sec == 1)
     def _():
         pl.semaphore_wait(go_sem, 1)
 
     pool_copy.wait()
-    for copy in pool_copies + own_pool:
+    pool_copies += value_copies
+    for copy in own_pool + pool_copies:
         copy.start()
 
     def arrived(dst, recv):
         remote(dst, dst, fin_send.at[0], recv, me, lax.rem(sec + 1, sections)).wait_recv()
 
-    for d in others:
-        src = peer(d)
-        arrived(meta.at[src], meta_recv.at[src])
-    counts[...] = jnp.zeros(counts.shape, f32)
-    for t in range(slots):
-        lines = slice(t * row_dev, (t + 1) * row_dev)
-        counts[lines, t * span_pad : (t + 1) * span_pad] = meta[t, :, :span_pad]
-        cos_v[lines, :] = meta[t, :, span_pad:]
-    spot = lax.broadcasted_iota(jnp.int32, (rows, HD), 1)
     half = HD // 2
-    pair = jnp.where(spot < half, spot, spot - half).astype(f32)
-    frequency = jnp.exp(pair * (-2.0 / HD) * jnp.log(jnp.full((rows, HD), rope_base, f32)))
-    angle = cos_v[...] * frequency
-    cosine = jnp.cos(angle)
-    sine = jnp.sin(angle) * jnp.where(spot < half, -1.0, 1.0)
-    cos_v[...] = cosine
-    sin_v[...] = sine
+
+    def tables():
+        for d in others:
+            src = peer(d)
+            arrived(meta.at[src], meta_recv.at[src])
+        counts[...] = jnp.zeros(counts.shape, f32)
+        for t in range(slots):
+            lines = slice(t * row_dev, (t + 1) * row_dev)
+            counts[lines, t * span_pad : (t + 1) * span_pad] = meta[t, :, :span_pad]
+            cos_v[lines, :] = meta[t, :, span_pad:]
+        spot = lax.broadcasted_iota(jnp.int32, (rows, HD), 1)
+        pair = jnp.where(spot < half, spot, spot - half).astype(f32)
+        frequency = jnp.exp(pair * (-2.0 / HD) * jnp.log(jnp.full((rows, HD), rope_base, f32)))
+        angle = cos_v[...] * frequency
+        cosine = jnp.cos(angle)
+        sine = jnp.sin(angle) * jnp.where(spot < half, -1.0, 1.0)
+        cos_v[...] = cosine
+        sin_v[...] = sine
+
+    pl.when(sec > 0)(tables)
 
     def rope(x):
         x = x.astype(f32)
@@ -417,12 +420,21 @@
 
         else:
             arrived(stream.at[src], st_recv.at[src])
+        if d == 1:
+
+            @pl.when(sec == 0)
+            def _():
+                pl.semaphore_signal(
+                    go_sem, inc=1, device_id={"tensor": me, "section": 1}, device_id_type=MESH
+                )
+
         start = pl.multiple_of(src * width, width)
         x = stream[src].astype(f32)
         square += jnp.sum(x * x, axis=1, keepdims=True)
         scaled = (x * gain[:, pl.ds(start, width)].astype(f32)).astype(bf16)
         q_sum += jnp.dot(scaled, wq_v[pl.ds(start, width), :], preferred_element_type=f32)
         kv_sum += jnp.dot(scaled, wkv_v[pl.ds(start, width), :], preferred_element_type=f32)
+    pl.when(sec == 0)(tables)
     inverse = lax.rsqrt(square * (1.0 / (slots * width)) + epsilon)
     query = rope((q_sum * inverse + bias[...].astype(f32)).astype(bf16))
     kv_new = (kv_sum * inverse).astype(bf16)
@@ -440,19 +452,10 @@
     for copy in fresh_copies:
         copy.start()
 
-    for copy in own_pool:
-        copy.wait()
+    own_pool[0].wait()
     for d in others:
         src = peer(d)
         arrived(keys.at[src, pl.ds(0, pages)], key_recv.at[src])
-        arrived(values.at[src, pl.ds(0, pages)], val_recv.at[src])
-
-    @pl.when(sec < last)
-    def _():
-        pl.semaphore_signal(
-            go_sem, inc=1, device_id={"tensor": me, "section": sec + 1}, device_id_type=MESH
-        )
-
     scaling = HD**-0.5
     times = counts[...]
     scores = (
@@ -467,6 +470,10 @@
     top = jnp.max(jnp.where(times > 0, scores, -1e30), axis=1, keepdims=True)
     weights = jnp.where(times > 0, times * jnp.exp(scores - top), 0.0)
     total = jnp.sum(weights, axis=1, keepdims=True)
+    own_pool[1].wait()
+    for d in others:
+        src = peer(d)
+        arrived(values.at[src, pl.ds(0, pages)], val_recv.at[src])
     mixed = jnp.dot(
         weights.astype(bf16),
         values[...].reshape(slots * span_pad, HD),
@@ -481,32 +488,40 @@
     for copy in part_copies:
         copy.start()
 
-    for d in others:
-        src = peer(d)
-        arrived(fresh.at[src], fresh_recv.at[src])
-
     def fresh_head(column):
         first = pl.multiple_of(HD + lax.rem(column, kv_cols), HD)
         return fresh[column // kv_cols, :, pl.ds(first, HD)].astype(f32)
 
-    own, fresh_values = [], []
+    reach = [
+        max(
+            ranked[m].index(t)
+            for m in range(slots)
+            for h in [ranked[m][k]]
+            for column in [(h // group) * HD]
+            for t in [h, column // kv_cols, (kv_half + column) // kv_cols]
+        )
+        for k in range(slots)
+    ]
+    summed = stream[me].astype(f32)
+    wo_copy.wait()
+    near_by = 0
     for k in range(slots):
         h = peer(k)
+        while near_by < reach[k]:
+            near_by += 1
+            arrived(fresh.at[peer(near_by)], fresh_recv.at[peer(near_by)])
         key = fresh_head((h // group) * HD)
-        own.append(
-            jnp.sum(fresh[h, :, :HD].astype(f32) * key, axis=1, keepdims=True) * scaling
-        )
-        fresh_values.append(fresh_head(kv_half + (h // group) * HD))
-    wo_copy.wait()
-    summed = stream[me].astype(f32)
-    for k in range(slots):
-        h = peer(k)
+        value = fresh_head(kv_half + (h // group) * HD)
+        own = jnp.sum(fresh[h, :, :HD].astype(f32) * key, axis=1, keepdims=True) * scaling
         if k:
             arrived(parts.at[h], part_recv.at[h])
-        share = 1.0 / (1.0 + jnp.exp(parts[h, :, HD:] - own[k]))
-        mixture = (parts[h, :, :HD] * (1.0 - share) + fresh_values[k] * share).astype(bf16)
+        share = 1.0 / (1.0 + jnp.exp(parts[h, :, HD:] - own))
+        mixture = (parts[h, :, :HD] * (1.0 - share) + value * share).astype(bf16)
         lines = pl.ds(pl.multiple_of(h * HD, HD), HD)
         summed += jnp.dot(mixture, wo_v[lines, :], preferred_element_type=f32)
+    while near_by < slots - 1:
+        near_by += 1
+        arrived(fresh.at[peer(near_by)], fresh_recv.at[peer(near_by)])
     new = summed.astype(bf16)
 
     def next_copies():
@@ -538,6 +553,11 @@
         out[...] = wide[last * out_rows :].astype(bf16)
         for j in range(last):
             fin_copy(j).wait_send()
+
+    @pl.when(sec == 0)
+    def _():
+        for copy in first_copies():
+            copy.wait_send()
 
     for copy in meta_copies + pool_copies + fresh_copies + part_copies:
         copy.wait_send()
@@ -557,7 +577,7 @@
     return pl.pallas_call(
         functools.partial(fused, slots, sections),
         out_shape=jax.ShapeDtypeStruct((rows // sections, width), bf16),
-        in_specs=[ANY] * 9,
+        in_specs=[HBM] * 9,
         out_specs=VMEM,
         scratch_shapes=[
             pltpu.VMEM(gain.shape, bf16),

time: 46.3 us -> 44.9 us (0.970)
  Pallas kernels: 44.8 us -> 43.4 us
    pallas_call x1, Pallas kernels: 44.8 us -> 43.4 us  [fused_shards(): pl.pallas_call(functools.partial(fused, slots, sections), out_shape=jax.S...]
where the time goes in v3:
time: 44.9 us; the launch traced here: 44.7 us
  Pallas kernels  43.4 us (97%)
  local copies, waits for them, and re-layouts  1.3 us (3%)
    pallas_call x1, Pallas kernels, fused_shards(): pl.pallas_call(functools.partial(fused, slots, sections), out_shape=jax.S...  43.4 us
    unnamed x1, local copies, waits for them, and re-layouts  1.3 us

profile of v3, /device:TPU:0, one launch (start us, length us, event | category | flops | bytes accessed | tf_op | source)
XLA Modules:
  0.0 44.7 jit_solution(16500631453718873400)
XLA Ops:
  0.0 43.4 %decode_stack.1 = bf16[2,2048]{1,0:T(2,128)(2,1)} custom-call(bf16[8,2048]{1,0:T(8,128)(2,1)} %hidden.1, bf16[1,8192]{1,0:T(2,128)(2,1)} %gain_in.1, bf16[1,8192,128]{2,1,0:T(8,128)(2,1)} %wq.1, bf16[1,128]{1,0:T(2,128)(2,1)} %bias_in.1, bf16[1,8192,256]{2,1,0:T(8,128)(2,1)} %wkv.1, bf16[1,512,2048]{2,1,0:T(8,128)(2,1)} %wo.1, ...), custom_call_target="tpu_custom_call" | custom-call | tf_op jit(solution)/shard_map/decode_stack/pallas_call | solution.py:577
  43.4 1.3 %copy.11 = bf16[2,2048]{1,0:T(2,128)(2,1)} copy(bf16[2,2048]{1,0:T(2,128)(2,1)} %decode_stack.1) | data formatting | bytes 16384
